TPU v7x, 32 devices: a whole 2x2x4 slice. The times are simulated.
32 devices in a mesh: pipe: 2 (over core), dp: 4 (over z), mp: 4 (over y, x).
Axes of the slice: x: 2, y: 2, z: 4, core: 2. Of those that a mesh axis runs over, the one named last changes fastest.
Arguments:
- hidden_states: bfloat16 [16, 64, 4096], P('dp'), may hold values from -6 to 6
- up_weight: bfloat16 [2, 4096, 7168], P('pipe', 'dp', 'mp'), may hold values from -0.09375 to 0.09375
- down_weight: bfloat16 [2, 7168, 4096], P('pipe', 'mp', 'dp'), may hold values from -0.0625 to 0.0625
- layer_gain: float32 [2, 4096], P('pipe'), may hold values from 0.5 to 1.5
- final_gain: float32 [4096], replicated, may hold values from 0.5 to 1.5
- unembedding: bfloat16 [32768, 4096], P(('pipe', 'mp')), may hold values from -32 to 32
- target_ids: int32 [16, 64], P('dp'), may hold values from 0 to 32767
- response_masks: int32 [16, 64], P('dp'), may hold values from 0 to 1, as said below
- anchor_logps: float32 [16, 64], P('dp'), may hold values from -14 to -10
- pairing: int32 [4, 4], P('dp'), may hold values from 0 to 3, each once within a row
Outputs:
- token_logps: float32 [16, 64], P('dp')
- seq_logps: float32 [16], P('dp')
- pair_losses: float32 [8], P('dp')
Inputs may be any that keep to these rules, and one draw needn't show every extreme that they name: response_masks is 1 on one unbroken run of at least one position per sequence, starting at or after position 8, and 0 elsewhere.
All inputs are finite; a program needn't handle non-finite values.
Results may differ from a plain program's by a relative error of at most 0.0075.
Values may be sent and summed in bfloat16 or wider, within the bound.
A program may use at most 192 MiB of HBM per device.

v0:
```python
import jax
import jax.numpy as jnp
from jax import lax
from jax.sharding import PartitionSpec as P

SEQ_MB = 1


epsilon = 1e-05
ipo_tau = 0.5


def from_behind(value, axis, steps):
    count = lax.axis_size(axis)
    pairs = [(source, (source + steps) % count) for source in range(count)]
    return lax.ppermute(value, axis, pairs)


def rms_scale(values, gain_row):
    mean_square = jnp.mean(values * values, axis=-1, keepdims=True)
    return values * lax.rsqrt(mean_square + epsilon) * gain_row


def shards(
    hidden_states,
    up_weight,
    down_weight,
    layer_gain,
    final_gain,
    unembedding,
    target_ids,
    response_masks,
    anchor_logps,
    pairing,
):
    seq_count, length, model_width = hidden_states.shape
    micro_count = seq_count // SEQ_MB
    batch_rows = SEQ_MB * length
    mask_values = response_masks.astype(jnp.float32)
    local_counts = jnp.sum(mask_values, axis=1)
    up_full, down_full = (
        lax.all_gather(up_weight, "dp", axis=1, tiled=True),
        lax.all_gather(down_weight, "dp", axis=2, tiled=True),
    )
    up_matrix = up_full[0]
    down_matrix = down_full[0]
    gain_row = layer_gain[0]
    section_index = lax.axis_index("pipe")

    def layer_partial(states):
        wide_states = states.astype(jnp.float32)
        normed = rms_scale(wide_states, gain_row).astype(jnp.bfloat16)
        active = jax.nn.silu(jnp.dot(normed, up_matrix, preferred_element_type=jnp.float32)).astype(
            jnp.bfloat16
        )
        return (wide_states, jnp.dot(active, down_matrix, preferred_element_type=jnp.float32))

    share_width = model_width // lax.axis_size("mp")
    column_start = lax.axis_index("mp") * share_width

    def run_layer(states):
        wide_states, partial_sum = layer_partial(states)
        summed = lax.psum_scatter(partial_sum, "mp", scatter_dimension=1, tiled=True)
        residual_share = lax.dynamic_slice_in_dim(wide_states, column_start, share_width, 1)
        return (residual_share + summed).astype(jnp.bfloat16)

    def widen(rows):
        return lax.all_gather(rows, "mp", axis=1, tiled=True)

    def advance(loop_state, step_index):
        incoming, finished = loop_state
        fresh_rows = lax.dynamic_index_in_dim(
            hidden_states, jnp.minimum(step_index, micro_count - 1), 0, keepdims=False
        )
        states = jnp.where(section_index == 0, fresh_rows, widen(incoming))
        output = run_layer(states)
        passed = from_behind(output, "pipe", 1)
        final_rows = jnp.where(section_index == 0, passed, output)
        slot_index = jnp.maximum(step_index - 1, 0)
        previous = lax.dynamic_index_in_dim(finished, slot_index, 0, keepdims=False)
        stored = jnp.where(step_index > 0, final_rows, previous)
        finished = lax.dynamic_update_index_in_dim(finished, stored, slot_index, 0)
        return ((passed, finished), None)

    start_state = (
        jnp.zeros((batch_rows, share_width), jnp.bfloat16),
        jnp.zeros((micro_count, batch_rows, share_width), jnp.bfloat16),
    )
    step_range = jnp.arange(micro_count + 1, dtype=jnp.int32)
    (unused_rows, finished), unused_out = lax.scan(advance, start_state, step_range)
    finals = widen(finished.reshape(seq_count * length, share_width))
    normed_final = rms_scale(finals.astype(jnp.float32), final_gain).astype(jnp.bfloat16)
    logits = lax.dot_general(
        normed_final, unembedding, (((1,), (1,)), ((), ())), preferred_element_type=jnp.float32
    )
    vocab_start = lax.axis_index(("pipe", "mp")) * unembedding.shape[0]
    local_ids = target_ids.reshape(-1) - vocab_start
    columns = lax.broadcasted_iota(jnp.int32, logits.shape, 1)
    picked = jnp.sum(jnp.where(columns == local_ids[:, None], logits, 0.0), axis=1)
    local_top = jnp.max(logits, axis=1)
    local_sum = jnp.sum(jnp.exp(logits - local_top[:, None]), axis=1)
    top_value = lax.pmax(local_top, ("pipe", "mp"))
    exp_total, picked_all = lax.psum(
        (local_sum * jnp.exp(local_top - top_value), picked), ("pipe", "mp")
    )
    token_logps = (picked_all - top_value - jnp.log(exp_total)).reshape(seq_count, length)

    def count_one(running, local_value):
        return (running, lax.psum(local_value, "dp"))

    unused_sum, counts = lax.scan(count_one, jnp.zeros((), jnp.float32), local_counts)
    mean_length = counts / (lax.axis_size("dp") * SEQ_MB)
    divisor = jnp.repeat(mean_length, SEQ_MB)
    policy = jnp.sum(mask_values * token_logps, axis=1) / divisor
    anchor = jnp.sum(mask_values * anchor_logps, axis=1) / divisor
    log_gaps = policy - anchor
    positions = jnp.arange(seq_count, dtype=jnp.int32)
    chosen = jnp.sum(
        jnp.where(pairing[0, 0::2][:, None] == positions[None, :], log_gaps[None, :], 0.0), axis=1
    )
    rejected = jnp.sum(
        jnp.where(pairing[0, 1::2][:, None] == positions[None, :], log_gaps[None, :], 0.0), axis=1
    )
    losses = (chosen - rejected - 0.5 / ipo_tau) ** 2
    return (token_logps, policy, losses)


def solution(mesh):
    return jax.shard_map(
        shards,
        mesh=mesh,
        in_specs=(
            P("dp", None, None),
            P("pipe", "dp", "mp"),
            P("pipe", "mp", "dp"),
            P("pipe", None),
            P(),
            P(("pipe", "mp"), None),
            P("dp", None),
            P("dp", None),
            P("dp", None),
            P("dp", None),
        ),
        out_specs=(P("dp", None), P("dp"), P("dp")),
        check_vma=False,
    )
```

profile of v0, /device:TPU:0, one launch (start us, length us, event | category | flops | bytes accessed | tf_op | source)
XLA Modules:
  0.0 956.5 jit_solution(14220361119281357036)
XLA Ops:
  8.7 256.1 %all-gather.4.cloned.1.call-done = bf16[1,4096,1792]{2,1,0:T(8,128)(2,1)} async-done(((bf16[1,1024,1792]{2,1,0:T(8,128)(2,1)}), bf16[1,4096,1792]{2,1,0:T(8,128)(2,1)}) %all-gather.4.cloned.1.call-update) | async-done | bytes 14680080 | tf_op jit(solution)/shard_map/all_gather | solution.py:42
  264.8 252.3 %all-gather.6.cloned.1.call-done = bf16[1,1792,4096]{2,1,0:T(8,128)(2,1)} async-done(((bf16[1,1792,1024]{2,1,0:T(8,128)(2,1)}), bf16[1,1792,4096]{2,1,0:T(8,128)(2,1)}) %all-gather.6.cloned.1.call-update) | async-done | bytes 14680080 | tf_op jit(solution)/shard_map/all_gather | solution.py:43
  517.2 294.7 %while.24 = (s32[]{:T(128)}, bf16[64,1024]{1,0:T(8,128)(2,1)S(1)}, bf16[4,64,1024]{2,1,0:T(8,128)(2,1)S(1)}, pred[]{:T(512)}, s32[5]{0:T(128)S(1)}, /*index=5*/b...) while((s32[]{:T(128)}, bf16[64,1024]{1,0:T(8,128)(2,1)S(1)}, ...), condition=%wide.region_3.4_spmd, body=%wide.region_0.3_spmd.sunk | while | flops 1881718912 | bytes 40125776 | solution.py:90
  518.4 10.0 %all_gather.19 = bf16[64,4096]{1,0:T(8,128)(2,1)S(1)} all-gather(bf16[64,1024]{1,0:T(8,128)(2,1)S(1)} %get-tuple-element.295), channel_id=1, replica_groups=mesh['pipe'=2,'dp'=4,'mp'=4] {'mp'}, dimensions={1}, use_global_device_ids=true | all-gather | bytes 655360 | tf_op jit(solution)/shard_map/while/body/eval_jaxpr/all_gather | solution.py:68
  529.8 15.9 %fusion.26 = f32[64,4096]{1,0:T(8,128)} fusion(bf16[1792,4096]{1,0:T(8,128)(2,1)} %get-tuple-element.319, bf16[4096,1792]{1,0:T(8,128)(2,1)} %get-tuple-element.318, f32[64,4096]{1,0:T(8,128)S(1)} %get-tuple-element.273, f32[4096]{0:T(1024)S(1)} %bitcast.42, f32[64]{0:T(128)S(1)} %add_rsqrt_fusion.3), kind=kOutput, calls=%fused_computation.8.clone.1 | convolution fusion | flops 1880408064 | bytes 31473920 | tf_op jit(solution)/shard_map/while/body/eval_jaxpr/dot_general | solution.py:56
  545.7 25.5 %reduce-scatter.2.cloned.1.call-done = f32[64,1024]{1,0:T(8,128)} async-done(((f32[64,4096]{1,0:T(8,128)}), f32[64,1024]{1,0:T(8,128)}) %reduce-scatter.2.cloned.1.call-update) | async-done | bytes 262160 | tf_op jit(solution)/shard_map/while/body/eval_jaxpr/reduce_scatter | solution.py:63
  574.9 10.5 %all_gather.19 = bf16[64,4096]{1,0:T(8,128)(2,1)S(1)} all-gather(bf16[64,1024]{1,0:T(8,128)(2,1)S(1)} %get-tuple-element.295), channel_id=1, replica_groups=mesh['pipe'=2,'dp'=4,'mp'=4] {'mp'}, dimensions={1}, use_global_device_ids=true | all-gather | bytes 655360 | tf_op jit(solution)/shard_map/while/body/eval_jaxpr/all_gather | solution.py:68
  585.4 1.3 multiply_reduce_fusion.4
  586.7 15.9 %fusion.26 = f32[64,4096]{1,0:T(8,128)} fusion(bf16[1792,4096]{1,0:T(8,128)(2,1)} %get-tuple-element.319, bf16[4096,1792]{1,0:T(8,128)(2,1)} %get-tuple-element.318, f32[64,4096]{1,0:T(8,128)S(1)} %get-tuple-element.273, f32[4096]{0:T(1024)S(1)} %bitcast.42, f32[64]{0:T(128)S(1)} %add_rsqrt_fusion.3), kind=kOutput, calls=%fused_computation.8.clone.1 | convolution fusion | flops 1880408064 | bytes 31473920 | tf_op jit(solution)/shard_map/while/body/eval_jaxpr/dot_general | solution.py:56
  602.7 28.1 %reduce-scatter.2.cloned.1.call-done = f32[64,1024]{1,0:T(8,128)} async-done(((f32[64,4096]{1,0:T(8,128)}), f32[64,1024]{1,0:T(8,128)}) %reduce-scatter.2.cloned.1.call-update) | async-done | bytes 262160 | tf_op jit(solution)/shard_map/while/body/eval_jaxpr/reduce_scatter | solution.py:63
  634.5 10.4 %all_gather.19 = bf16[64,4096]{1,0:T(8,128)(2,1)S(1)} all-gather(bf16[64,1024]{1,0:T(8,128)(2,1)S(1)} %get-tuple-element.295), channel_id=1, replica_groups=mesh['pipe'=2,'dp'=4,'mp'=4] {'mp'}, dimensions={1}, use_global_device_ids=true | all-gather | bytes 655360 | tf_op jit(solution)/shard_map/while/body/eval_jaxpr/all_gather | solution.py:68
  646.3 15.9 %fusion.26 = f32[64,4096]{1,0:T(8,128)} fusion(bf16[1792,4096]{1,0:T(8,128)(2,1)} %get-tuple-element.319, bf16[4096,1792]{1,0:T(8,128)(2,1)} %get-tuple-element.318, f32[64,4096]{1,0:T(8,128)S(1)} %get-tuple-element.273, f32[4096]{0:T(1024)S(1)} %bitcast.42, f32[64]{0:T(128)S(1)} %add_rsqrt_fusion.3), kind=kOutput, calls=%fused_computation.8.clone.1 | convolution fusion | flops 1880408064 | bytes 31473920 | tf_op jit(solution)/shard_map/while/body/eval_jaxpr/dot_general | solution.py:56
  662.2 28.1 %reduce-scatter.2.cloned.1.call-done = f32[64,1024]{1,0:T(8,128)} async-done(((f32[64,4096]{1,0:T(8,128)}), f32[64,1024]{1,0:T(8,128)}) %reduce-scatter.2.cloned.1.call-update) | async-done | bytes 262160 | tf_op jit(solution)/shard_map/while/body/eval_jaxpr/reduce_scatter | solution.py:63
  694.0 10.5 %all_gather.19 = bf16[64,4096]{1,0:T(8,128)(2,1)S(1)} all-gather(bf16[64,1024]{1,0:T(8,128)(2,1)S(1)} %get-tuple-element.295), channel_id=1, replica_groups=mesh['pipe'=2,'dp'=4,'mp'=4] {'mp'}, dimensions={1}, use_global_device_ids=true | all-gather | bytes 655360 | tf_op jit(solution)/shard_map/while/body/eval_jaxpr/all_gather | solution.py:68
  704.5 1.3 multiply_reduce_fusion.4
  705.8 15.9 %fusion.26 = f32[64,4096]{1,0:T(8,128)} fusion(bf16[1792,4096]{1,0:T(8,128)(2,1)} %get-tuple-element.319, bf16[4096,1792]{1,0:T(8,128)(2,1)} %get-tuple-element.318, f32[64,4096]{1,0:T(8,128)S(1)} %get-tuple-element.273, f32[4096]{0:T(1024)S(1)} %bitcast.42, f32[64]{0:T(128)S(1)} %add_rsqrt_fusion.3), kind=kOutput, calls=%fused_computation.8.clone.1 | convolution fusion | flops 1880408064 | bytes 31473920 | tf_op jit(solution)/shard_map/while/body/eval_jaxpr/dot_general | solution.py:56
  721.8 28.1 %reduce-scatter.2.cloned.1.call-done = f32[64,1024]{1,0:T(8,128)} async-done(((f32[64,4096]{1,0:T(8,128)}), f32[64,1024]{1,0:T(8,128)}) %reduce-scatter.2.cloned.1.call-update) | async-done | bytes 262160 | tf_op jit(solution)/shard_map/while/body/eval_jaxpr/reduce_scatter | solution.py:63
  753.6 10.5 %all_gather.19 = bf16[64,4096]{1,0:T(8,128)(2,1)S(1)} all-gather(bf16[64,1024]{1,0:T(8,128)(2,1)S(1)} %get-tuple-element.295), channel_id=1, replica_groups=mesh['pipe'=2,'dp'=4,'mp'=4] {'mp'}, dimensions={1}, use_global_device_ids=true | all-gather | bytes 655360 | tf_op jit(solution)/shard_map/while/body/eval_jaxpr/all_gather | solution.py:68
  764.1 1.3 multiply_reduce_fusion.4
  765.4 15.9 %fusion.26 = f32[64,4096]{1,0:T(8,128)} fusion(bf16[1792,4096]{1,0:T(8,128)(2,1)} %get-tuple-element.319, bf16[4096,1792]{1,0:T(8,128)(2,1)} %get-tuple-element.318, f32[64,4096]{1,0:T(8,128)S(1)} %get-tuple-element.273, f32[4096]{0:T(1024)S(1)} %bitcast.42, f32[64]{0:T(128)S(1)} %add_rsqrt_fusion.3), kind=kOutput, calls=%fused_computation.8.clone.1 | convolution fusion | flops 1880408064 | bytes 31473920 | tf_op jit(solution)/shard_map/while/body/eval_jaxpr/dot_general | solution.py:56
  781.3 28.1 %reduce-scatter.2.cloned.1.call-done = f32[64,1024]{1,0:T(8,128)} async-done(((f32[64,4096]{1,0:T(8,128)}), f32[64,1024]{1,0:T(8,128)}) %reduce-scatter.2.cloned.1.call-update) | async-done | bytes 262160 | tf_op jit(solution)/shard_map/while/body/eval_jaxpr/reduce_scatter | solution.py:63
  813.0 36.9 %all-gather.8.cloned.1.call-done = bf16[256,4096]{1,0:T(8,128)(2,1)} async-done(((bf16[256,1024]{1,0:T(8,128)(2,1)}), bf16[256,4096]{1,0:T(8,128)(2,1)}) %all-gather.8.cloned.1.call-update) | async-done | bytes 2097168 | tf_op jit(solution)/shard_map/all_gather | solution.py:68
  849.8 2.1 fusion.7
  851.9 17.6 %fusion.17 = (f32[256]{0:T(256)S(1)}, f32[256,4096]{1,0:T(8,128)}) fusion(bf16[4096,4096]{1,0:T(8,128)(2,1)} %param.19, bf16[256,4096]{1,0:T(8,128)(2,1)} %all-gather.8.cloned.1.call-done, f32[4096]{0:T(1024)S(1)} %copy-done.6, f32[256]{0:T(256)S(1)} %add_rsqrt_fusion.1), kind=kOutput, calls=%fused_computation.41 | convolution fusion | flops 8595177472 | bytes 39864320 | tf_op jit(solution)/shard_map/dot_general | solution.py:93
  869.5 14.4 %pmax.7 = f32[256]{0:T(256)S(1)} all-reduce(f32[256]{0:T(256)S(1)} %get-tuple-element.192), channel_id=1, replica_groups=mesh['pipe'=2,'dp'=4,'mp'=4] {'pipe','mp'}, use_global_device_ids=true, to_apply=%region_8.9 | all-reduce | flops 256 | bytes 2048 | tf_op jit(solution)/shard_map/pmax | solution.py:102
  883.9 3.5 select_reduce_fusion
  887.4 14.2 %all-reduce = (f32[256]{0:T(256)S(1)}, f32[256]{0:T(256)S(1)}) all-reduce(f32[256]{0:T(256)S(1)} %exponential_multiply_fusion, f32[256]{0:T(256)S(1)} %get-tuple-element.153), channel_id=1, replica_groups=mesh['pipe'=2,'dp'=4,'mp'=4] {'pipe','mp'}, use_global_device_ids=true, to_apply=%region_10.11 | all-reduce | flops 512 | bytes 4096 | tf_op jit(solution)/shard_map/psum | solution.py:103
  901.8 46.6 %while.25 = (s32[]{:T(128)}, f32[4]{0:T(128)S(1)}, f32[4]{0:T(128)S(1)}, s32[]{:T(128)}) while((s32[]{:T(128)}, f32[4]{0:T(128)S(1)}, f32[4]{0:T(128)S(1)}, s32[]{:T(128)}) %tuple.55), condition=%wide.region_15.16_spmd, body=%wide.region_13.15_spmd.sunk | while | flops 3 | bytes 85 | solution.py:111
  902.4 12.3 %psum.24 = f32[1]{0:T(128)} all-reduce(f32[1]{0:T(128)} %dynamic_slice.42), channel_id=1, replica_groups=mesh['pipe'=2,'dp'=4,'mp'=4] {'dp'}, use_global_device_ids=true, to_apply=%region_14.14 | all-reduce | flops 1 | bytes 8 | tf_op jit(solution)/shard_map/while/body/eval_jaxpr/psum | solution.py:109
  916.1 9.0 psum.24
  926.4 11.0 %psum.24 = f32[1]{0:T(128)} all-reduce(f32[1]{0:T(128)} %dynamic_slice.42), channel_id=1, replica_groups=mesh['pipe'=2,'dp'=4,'mp'=4] {'dp'}, use_global_device_ids=true, to_apply=%region_14.14 | all-reduce | flops 1 | bytes 8 | tf_op jit(solution)/shard_map/while/body/eval_jaxpr/psum | solution.py:109
  938.7 9.0 psum.24
  (93 shorter events, 21.4 us)
Async XLA Ops:
  7.2 510.0 %copy-start.1 = (f32[1,4096]{1,0:T(1,128)S(1)}, f32[1,4096]{1,0:T(1,128)}, u32[]{:S(2)}) copy-start(f32[1,4096]{1,0:T(1,128)} %param.17) | copy-start | bytes 49156
  7.2 257.6 %all-gather.4.cloned.1.call-start = ((), (), s32[]{:S(2)}) async-start(), calls=%async_computation.1 | async-start | bytes 18350080 | tf_op jit(solution)/shard_map/all_gather | solution.py:42
  7.9 509.1 %all-gather.6.cloned.1.call-start = ((), (), s32[]{:S(2)}) async-start(), calls=%async_computation.2 | async-start | bytes 18350080 | tf_op jit(solution)/shard_map/all_gather | solution.py:43
  517.1 295.6 %copy-start.7 = (s32[1,4]{1,0:T(1,128)S(1)}, s32[1,4]{1,0:T(1,128)}, u32[]{:S(2)}) copy-start(s32[1,4]{1,0:T(1,128)} %param.23) | copy-start | bytes 52
  517.1 295.7 %copy-start.3 = (s32[4,64]{1,0:T(4,128)S(1)}, s32[4,64]{1,0:T(4,128)}, u32[]{:S(2)}) copy-start(s32[4,64]{1,0:T(4,128)} %param.20) | copy-start | bytes 3076
  517.2 334.8 %copy-start.6 = (f32[4096]{0:T(1024)S(1)}, f32[4096]{0:T(1024)}, u32[]{:S(2)}) copy-start(f32[4096]{0:T(1024)} %param.18) | copy-start | bytes 49156
  517.2 54.0 %reduce-scatter.2.cloned.1.call-start = ((), (), s32[]{:S(2)}) async-start(), calls=%async_computation.4 | async-start | bytes 1310720 | tf_op jit(solution)/shard_map/while/body/eval_jaxpr/reduce_scatter | solution.py:63
  572.2 1.4 collective-permute-start
  573.6 57.1 %reduce-scatter.2.cloned.1.call-start = ((), (), s32[]{:S(2)}) async-start(), calls=%async_computation.4 | async-start | bytes 1310720 | tf_op jit(solution)/shard_map/while/body/eval_jaxpr/reduce_scatter | solution.py:63
  631.7 1.4 collective-permute-start
  633.2 57.1 %reduce-scatter.2.cloned.1.call-start = ((), (), s32[]{:S(2)}) async-start(), calls=%async_computation.4 | async-start | bytes 1310720 | tf_op jit(solution)/shard_map/while/body/eval_jaxpr/reduce_scatter | solution.py:63
  691.3 1.4 collective-permute-start
  692.7 57.1 %reduce-scatter.2.cloned.1.call-start = ((), (), s32[]{:S(2)}) async-start(), calls=%async_computation.4 | async-start | bytes 1310720 | tf_op jit(solution)/shard_map/while/body/eval_jaxpr/reduce_scatter | solution.py:63
  750.8 1.4 collective-permute-start
  752.3 57.1 %reduce-scatter.2.cloned.1.call-start = ((), (), s32[]{:S(2)}) async-start(), calls=%async_computation.4 | async-start | bytes 1310720 | tf_op jit(solution)/shard_map/while/body/eval_jaxpr/reduce_scatter | solution.py:63
  810.4 1.4 collective-permute-start
  811.9 0.8 copy-start
  811.9 38.0 %all-gather.8.cloned.1.call-start = ((), (), s32[]{:S(2)}) async-start(), calls=%async_computation.3 | async-start | bytes 2621440 | tf_op jit(solution)/shard_map/all_gather | solution.py:68
  869.5 32.2 %copy-start.4 = (f32[4,64]{1,0:T(4,128)S(1)}, f32[4,64]{1,0:T(4,128)}, u32[]{:S(2)}) copy-start(f32[4,64]{1,0:T(4,128)} %param.22) | copy-start | bytes 3076
  869.5 32.2 %copy-start.5 = (s32[4,64]{1,0:T(4,128)S(1)}, s32[4,64]{1,0:T(4,128)}, u32[]{:S(2)}) copy-start(s32[4,64]{1,0:T(4,128)} %param.21) | copy-start | bytes 3076
  901.7 48.0 %copy-start.2 = (f32[4,64]{1,0:T(4,128)}, f32[4,64]{1,0:T(4,128)S(1)}, u32[]{:S(2)}) copy-start(f32[4,64]{1,0:T(4,128)S(1)} %reshape.51) | copy-start | bytes 3076
Sparse Core Ops, SparseCore 0:
  9.5 255.1 all-gather.3
  266.3 250.6 all-gather.5
  545.9 25.2 reduce-scatter.1
  602.8 27.9 reduce-scatter.1
  662.3 27.8 reduce-scatter.1
  721.9 27.9 reduce-scatter.1
  781.5 27.8 reduce-scatter.1
  814.5 35.2 all-gather.7
where the time goes:
time: 958 us; the launch traced here: 957 us
  waiting for transfers between devices  685 us (72%)
  blocking collectives  122 us (13%)
  matrix products  97.2 us (10%)
  other arithmetic  18.7 us (2%)
  between operations  14.2 us (1%)
  loops' own time  9.63 us (1%)
  local copies, waits for them, and re-layouts  9.59 us (1%)
    all_gather x1, waiting for transfers between devices, shards(): lax.all_gather(up_weight, 'dp', axis=1, tiled=True)  256 us
    all_gather x1, waiting for transfers between devices, shards(): lax.all_gather(down_weight, 'dp', axis=2, tiled=True)  252 us
    reduce_scatter x5, waiting for transfers between devices, run_layer(): lax.psum_scatter(partial_sum, 'mp', scatter_dimension=1, tiled=True)  138 us
    dot_general x5, matrix products, layer_partial(): jnp.dot(active, down_matrix, preferred_element_type=jnp.float32)  79.7 us
    all_gather x5, blocking collectives, widen(): return lax.all_gather(rows, 'mp', axis=1, tiled=True)  51.9 us
    psum x4, blocking collectives, count_one(): return (running, lax.psum(local_value, 'dp'))  41.2 us
    all_gather x1, waiting for transfers between devices, widen(): return lax.all_gather(rows, 'mp', axis=1, tiled=True)  36.9 us
  transfers between devices with their start and end apart: 13, of which 13 were waited for; matrix products, arithmetic and copies ran while one was open for 0% of the time, Pallas kernels for 0%

commit v1 on v0

v1 whole, which is shorter than its diff:
```python
import jax
import jax.numpy as jnp
from jax import lax
from jax.sharding import PartitionSpec as P

SEQ_MB = 1

epsilon = 1e-05
ipo_tau = 0.5
VP = ("pipe", "mp")


def shards(
    hidden_states,
    up_weight,
    down_weight,
    layer_gain,
    final_gain,
    unembedding,
    target_ids,
    response_masks,
    anchor_logps,
    pairing,
):
    seq_count, length, model_width = hidden_states.shape
    groups = lax.axis_size("dp")
    vp_size = lax.axis_size("pipe") * lax.axis_size("mp")
    vp_index = lax.axis_index(VP)
    dp_index = lax.axis_index("dp")
    pipe_index = lax.axis_index("pipe")
    rows = seq_count * length
    part = rows // vp_size
    block = model_width // groups
    mask_values = response_masks.astype(jnp.float32)
    local_counts = jnp.sum(mask_values, axis=1)
    counts = lax.psum(local_counts, "dp")

    up_own, down_own = up_weight[0], down_weight[0]
    half = up_own.shape[1] // 2
    away = (1 - pipe_index) * half
    keep = pipe_index * half
    swap = [(0, 1), (1, 0)]
    gain_other = lax.ppermute(layer_gain, "pipe", swap)
    up_other = lax.ppermute(lax.dynamic_slice_in_dim(up_own, away, half, 1), "pipe", swap)
    down_other = lax.ppermute(lax.dynamic_slice_in_dim(down_own, away, half, 0), "pipe", swap)
    up_mine = lax.dynamic_slice_in_dim(up_own, keep, half, 1)
    down_mine = lax.dynamic_slice_in_dim(down_own, keep, half, 0)

    def section_of(s):
        own = pipe_index == s
        gain = jnp.where(own, layer_gain[0], gain_other[0])
        return (
            lax.dynamic_slice_in_dim(gain, dp_index * block, block, 0),
            jnp.where(own, up_mine, up_other),
            jnp.where(own, down_mine, down_other),
        )

    mine = lax.dynamic_slice_in_dim(
        hidden_states.reshape(rows, model_width), vp_index * part, part, 0
    )
    blocks = lax.all_to_all(
        mine.reshape(part, groups, block).transpose(1, 0, 2), "dp", 0, 0, tiled=True
    ).reshape(groups * part, block)

    for s in range(2):
        gain, up, down = section_of(s)
        wide = blocks.astype(jnp.float32)
        total = lax.psum(jnp.sum(wide * wide, axis=1, keepdims=True), "dp")
        normed = (wide * lax.rsqrt(total / model_width + epsilon) * gain).astype(jnp.bfloat16)
        full = lax.all_gather(normed, VP, axis=0, tiled=True)
        hidden = jnp.dot(full, up, preferred_element_type=jnp.float32).astype(jnp.bfloat16)
        hidden = lax.psum_scatter(hidden, "dp", scatter_dimension=0, tiled=True)
        active = jax.nn.silu(hidden.astype(jnp.float32)).astype(jnp.bfloat16)
        active = lax.all_gather(active, "dp", axis=0, tiled=True)
        out = jnp.dot(active, down, preferred_element_type=jnp.float32).astype(jnp.bfloat16)
        out = lax.psum_scatter(out, VP, scatter_dimension=0, tiled=True)
        blocks = (wide + out.astype(jnp.float32)).astype(jnp.bfloat16)

    finals = lax.all_to_all(blocks.reshape(groups, part, block), "dp", 0, 0, tiled=True)
    finals = finals.transpose(1, 0, 2).reshape(part, model_width).astype(jnp.float32)
    mean_square = jnp.mean(finals * finals, axis=-1, keepdims=True)
    normed_final = (finals * lax.rsqrt(mean_square + epsilon) * final_gain).astype(jnp.bfloat16)
    normed_final = lax.all_gather(normed_final, VP, axis=0, tiled=True)
    logits = lax.dot_general(
        normed_final, unembedding, (((1,), (1,)), ((), ())), preferred_element_type=jnp.float32
    )
    vocab_start = vp_index * unembedding.shape[0]
    local_ids = target_ids.reshape(-1) - vocab_start
    columns = lax.broadcasted_iota(jnp.int32, logits.shape, 1)
    picked = jnp.sum(jnp.where(columns == local_ids[:, None], logits, 0.0), axis=1)
    local_top = jnp.max(logits, axis=1)
    local_sum = jnp.sum(jnp.exp(logits - local_top[:, None]), axis=1)
    stats = lax.all_gather(jnp.stack([local_top, local_sum, picked]), VP, axis=0)
    top_value = jnp.max(stats[:, 0], axis=0)
    exp_total = jnp.sum(stats[:, 1] * jnp.exp(stats[:, 0] - top_value), axis=0)
    picked_all = jnp.sum(stats[:, 2], axis=0)
    token_logps = (picked_all - top_value - jnp.log(exp_total)).reshape(seq_count, length)

    divisor = jnp.repeat(counts / (groups * SEQ_MB), SEQ_MB)
    policy = jnp.sum(mask_values * token_logps, axis=1) / divisor
    anchor = jnp.sum(mask_values * anchor_logps, axis=1) / divisor
    log_gaps = policy - anchor
    positions = jnp.arange(seq_count, dtype=jnp.int32)
    chosen = jnp.sum(
        jnp.where(pairing[0, 0::2][:, None] == positions[None, :], log_gaps[None, :], 0.0), axis=1
    )
    rejected = jnp.sum(
        jnp.where(pairing[0, 1::2][:, None] == positions[None, :], log_gaps[None, :], 0.0), axis=1
    )
    losses = (chosen - rejected - 0.5 / ipo_tau) ** 2
    return (token_logps, policy, losses)


def solution(mesh):
    return jax.shard_map(
        shards,
        mesh=mesh,
        in_specs=(
            P("dp", None, None),
            P("pipe", "dp", "mp"),
            P("pipe", "mp", "dp"),
            P("pipe", None),
            P(),
            P(("pipe", "mp"), None),
            P("dp", None),
            P("dp", None),
            P("dp", None),
            P("dp", None),
        ),
        out_specs=(P("dp", None), P("dp"), P("dp")),
        check_vma=False,
    )
```

time: 958 us -> 478 us (0.50)
  waiting for transfers between devices: 685 us -> 323 us
  matrix products: 97.2 us -> 41.6 us
  blocking collectives: 122 us -> 69.7 us
  loops' own time: 9.63 us -> 0 us
    all_gather x3 -> x5, waiting for transfers between devices: 545 us -> 147 us  [the longest x2 75.3 us: shards(): active = lax.all_gather(active, 'dp', axis=0, tiled=True)]
    dot_general x5 -> x4, matrix products: 79.7 us -> 24.1 us  [the longest x2 12.1 us: shards(): jnp.dot(active, down, preferred_element_type=jnp.float32)]
    all_gather x5 -> x1, blocking collectives: 51.9 us -> 23.4 us  [shards(): lax.all_gather(jnp.stack([local_top, local_sum, picked]), VP, axis=0)]
    psum x5 -> x3, blocking collectives: 55.4 us -> 33.2 us  [the longest x2 21.5 us: shards(): total = lax.psum(jnp.sum(wide * wide, axis=1, keepdims=True), 'dp')]
    reduce_scatter x5 -> x4, waiting for transfers between devices: 138 us -> 160 us  [the longest x2 80.2 us: shards(): out = lax.psum_scatter(out, VP, scatter_dimension=0, tiled=True)]
    pmax x1 -> x0, blocking collectives: 14.4 us -> none  [shards(): top_value = lax.pmax(local_top, ('pipe', 'mp'))]
    all_to_all x0 -> x1, blocking collectives: none -> 13.1 us  [shards(): lax.all_to_all(blocks.reshape(groups, part, block), 'dp', 0, 0, tiled=True)]
    another operation x2 -> x0, loops' own time: 9.63 us -> none  [the longest x1 9.61 us: shards(): lax.scan(advance, start_state, step_range)]
  transfers between devices with their start and end apart: 13 -> 13, of which waited for: 13 -> 13; matrix products, arithmetic and copies ran while one was open for 0% -> 1% of each run, Pallas kernels for 0% -> 0%
where the time goes in v1:
time: 478 us; the launch traced here: 477 us
  waiting for transfers between devices  323 us (68%)
  blocking collectives  69.7 us (15%)
  matrix products  41.6 us (9%)
  other arithmetic  15.1 us (3%)
  between operations  14 us (3%)
  starting transfers between devices  6.89 us (1%)
  local copies, waits for them, and re-layouts  6.37 us (1%)
    reduce_scatter x2, waiting for transfers between devices, shards(): out = lax.psum_scatter(out, VP, scatter_dimension=0, tiled=True)  80.2 us
    reduce_scatter x2, waiting for transfers between devices, shards(): hidden = lax.psum_scatter(hidden, 'dp', scatter_dimension=0, tiled=True)  79.6 us
    all_gather x2, waiting for transfers between devices, shards(): active = lax.all_gather(active, 'dp', axis=0, tiled=True)  75.3 us
    all_gather x2, waiting for transfers between devices, shards(): full = lax.all_gather(normed, VP, axis=0, tiled=True)  45.6 us
    all_gather x1, waiting for transfers between devices, shards(): normed_final = lax.all_gather(normed_final, VP, axis=0, tiled=True)  25.8 us
    all_gather x1, blocking collectives, shards(): lax.all_gather(jnp.stack([local_top, local_sum, picked]), VP, axis=0)  23.4 us
    psum x2, blocking collectives, shards(): total = lax.psum(jnp.sum(wide * wide, axis=1, keepdims=True), 'dp')  21.5 us
    dot_general x1, matrix products, shards(): lax.dot_general(normed_final, unembedding, (((1,), (1,)), ((), ())), pref...  17.5 us
  transfers between devices with their start and end apart: 13, of which 13 were waited for; matrix products, arithmetic and copies ran while one was open for 1% of the time, Pallas kernels for 0%

profile of v1, /device:TPU:0, one launch (start us, length us, event | category | flops | bytes accessed | tf_op | source)
XLA Modules:
  0.0 476.9 jit_solution(5954369776052634757)
XLA Ops:
  7.2 1.6 copy-done
  9.7 6.3 %all-to-all-start = ((bf16[4,32,1024]{2,1,0:T(8,128)(2,1)}), bf16[4,32,1024]{2,1,0:T(8,128)(2,1)S(1)}, u32[]{:S(2)}, u32[]{:S(2)}) async-start(bf16[4,32,1024]{2,1,0:T(8,128)(2,1)} %copy.22), calls=%async_computation | async-start | bytes 524288 | tf_op jit(solution)/shard_map/all_to_all | solution.py:61
  16.2 1.2 collective-permute-done
  17.4 7.6 %all-to-all-done = bf16[4,32,1024]{2,1,0:T(8,128)(2,1)S(1)} async-done(((bf16[4,32,1024]{2,1,0:T(8,128)(2,1)}), bf16[4,32,1024]{2,1,0:T(8,128)(2,1)S(1)}, u32[]{:S(2)}, u32[]{:S(2)}) %all-to-all-start) | async-done | bytes 262176 | tf_op jit(solution)/shard_map/all_to_all | solution.py:61
  25.2 9.8 %psum.21 = f32[128,1]{0,1:T(1,128)S(1)} all-reduce(f32[128,1]{0,1:T(1,128)S(1)} %broadcast_in_dim.37), channel_id=1, replica_groups=mesh['pipe'=2,'dp'=4,'mp'=4] {'dp'}, use_global_device_ids=true, to_apply=%region_1.0 | all-reduce | flops 128 | bytes 1024 | tf_op jit(solution)/shard_map/psum | solution.py:68
  35.9 1.7 dynamic-slice_bitcast_fusion.1
  37.7 3.9 collective-permute-done.1
  41.6 20.5 %all-gather.8.cloned.1.call-done = bf16[1024,1024]{1,0:T(8,128)(2,1)} async-done(((bf16[128,1024]{1,0:T(8,128)(2,1)}), bf16[1024,1024]{1,0:T(8,128)(2,1)}) %all-gather.8.cloned.1.call-update) | async-done | bytes 2097168 | tf_op jit(solution)/shard_map/all_gather | solution.py:70
  62.0 5.7 %fusion.7 = bf16[1024,896]{1,0:T(8,128)(2,1)} fusion(bf16[1024,1024]{1,0:T(8,128)(2,1)} %all-gather.8.cloned.1.call-done, bf16[1024,896]{1,0:T(8,128)(2,1)} %collective-permute-done.1, pred[]{:T(512)S(6)} %eq.44, bf16[1,1024,1792]{2,1,0:T(8,128)(2,1)} %param.11, s32[]{:T(128)S(6)} %select_n.75), kind=kOutput, calls=%fused_computation.18 | convolution fusion | flops 1880883200 | bytes 7602181 | tf_op jit(solution)/shard_map/dot_general | solution.py:71
  67.9 40.0 %reduce-scatter.5.cloned.1.call-done = bf16[256,896]{1,0:T(8,128)(2,1)} async-done(((bf16[1024,896]{1,0:T(8,128)(2,1)}), bf16[256,896]{1,0:T(8,128)(2,1)}) %reduce-scatter.5.cloned.1.call-update) | async-done | bytes 458768 | tf_op jit(solution)/shard_map/reduce_scatter | solution.py:72
  107.9 2.1 fusion.15
  110.0 1.7 dynamic-slice_bitcast_fusion
  111.8 3.9 collective-permute-done.2
  115.7 34.8 %all-gather.10.cloned.1.call-done = bf16[1024,896]{1,0:T(8,128)(2,1)} async-done(((bf16[256,896]{1,0:T(8,128)(2,1)}), bf16[1024,896]{1,0:T(8,128)(2,1)}) %all-gather.10.cloned.1.call-update) | async-done | bytes 1835024 | tf_op jit(solution)/shard_map/all_gather | solution.py:74
  150.5 5.8 %convolution_convert_fusion.1 = bf16[1024,1024]{1,0:T(8,128)(2,1)} fusion(bf16[1024,896]{1,0:T(8,128)(2,1)} %all-gather.10.cloned.1.call-done, bf16[896,1024]{1,0:T(8,128)(2,1)} %collective-permute-done.2, pred[]{:T(512)S(6)} %eq.44, bf16[1,1792,1024]{2,1,0:T(8,128)(2,1)} %param.12, s32[]{:T(128)S(6)} %select_n.75), kind=kOutput, calls=%fused_computation.4 | convolution fusion | flops 1881014272 | bytes 7602181 | tf_op jit(solution)/shard_map/dot_general | solution.py:75
  156.3 40.2 %reduce-scatter.7.cloned.1.call-done = bf16[128,1024]{1,0:T(8,128)(2,1)} async-done(((bf16[1024,1024]{1,0:T(8,128)(2,1)}), bf16[128,1024]{1,0:T(8,128)(2,1)}) %reduce-scatter.7.cloned.1.call-update) | async-done | bytes 262160 | tf_op jit(solution)/shard_map/reduce_scatter | solution.py:76
  196.5 1.1 fusion.21
  197.6 11.7 %psum.22 = f32[128,1]{0,1:T(1,128)S(1)} all-reduce(f32[128,1]{0,1:T(1,128)S(1)} %bitcast.81), channel_id=1, replica_groups=mesh['pipe'=2,'dp'=4,'mp'=4] {'dp'}, use_global_device_ids=true, to_apply=%region_5.6 | all-reduce | flops 128 | bytes 1024 | tf_op jit(solution)/shard_map/psum | solution.py:68
  209.3 1.8 fusion.23
  211.2 25.1 %all-gather.12.cloned.1.call-done = bf16[1024,1024]{1,0:T(8,128)(2,1)} async-done(((bf16[128,1024]{1,0:T(8,128)(2,1)}), bf16[1024,1024]{1,0:T(8,128)(2,1)}) %all-gather.12.cloned.1.call-update) | async-done | bytes 2097168 | tf_op jit(solution)/shard_map/all_gather | solution.py:70
  236.3 6.3 %fusion.6 = bf16[1024,896]{1,0:T(8,128)(2,1)} fusion(bf16[1024,1024]{1,0:T(8,128)(2,1)} %all-gather.12.cloned.1.call-done, bf16[1024,896]{1,0:T(8,128)(2,1)} %collective-permute-done.1, pred[]{:T(512)S(6)} %eq.45, bf16[1,1024,1792]{2,1,0:T(8,128)(2,1)} %param.11, s32[]{:T(128)S(6)} %select_n.75), kind=kOutput, calls=%fused_computation.17 | convolution fusion | flops 1880883200 | bytes 7602181 | tf_op jit(solution)/shard_map/dot_general | solution.py:71
  242.7 39.6 %reduce-scatter.9.cloned.1.call-done = bf16[256,896]{1,0:T(8,128)(2,1)} async-done(((bf16[1024,896]{1,0:T(8,128)(2,1)}), bf16[256,896]{1,0:T(8,128)(2,1)}) %reduce-scatter.9.cloned.1.call-update) | async-done | bytes 458768 | tf_op jit(solution)/shard_map/reduce_scatter | solution.py:72
  282.3 2.1 fusion.19
  284.4 40.5 %all-gather.14.cloned.1.call-done = bf16[1024,896]{1,0:T(8,128)(2,1)} async-done(((bf16[256,896]{1,0:T(8,128)(2,1)}), bf16[1024,896]{1,0:T(8,128)(2,1)}) %all-gather.14.cloned.1.call-update) | async-done | bytes 1835024 | tf_op jit(solution)/shard_map/all_gather | solution.py:74
  324.9 6.3 %convolution_convert_fusion = bf16[1024,1024]{1,0:T(8,128)(2,1)} fusion(bf16[1024,896]{1,0:T(8,128)(2,1)} %all-gather.14.cloned.1.call-done, bf16[896,1024]{1,0:T(8,128)(2,1)} %collective-permute-done.2, pred[]{:T(512)S(6)} %eq.45, bf16[1,1792,1024]{2,1,0:T(8,128)(2,1)} %param.12, s32[]{:T(128)S(6)} %select_n.75), kind=kOutput, calls=%fused_computation.3 | convolution fusion | flops 1881014272 | bytes 7602181 | tf_op jit(solution)/shard_map/dot_general | solution.py:75
  331.3 40.0 %reduce-scatter.11.cloned.1.call-done = bf16[128,1024]{1,0:T(8,128)(2,1)} async-done(((bf16[1024,1024]{1,0:T(8,128)(2,1)}), bf16[128,1024]{1,0:T(8,128)(2,1)}) %reduce-scatter.11.cloned.1.call-update) | async-done | bytes 262160 | tf_op jit(solution)/shard_map/reduce_scatter | solution.py:76
  372.4 13.1 %all_to_all.10 = bf16[4,32,1024]{2,1,0:T(8,128)(2,1)S(1)} all-to-all(bf16[4,32,1024]{2,1,0:T(8,128)(2,1)S(1)} %bitcast.75), channel_id=1, replica_groups=mesh['pipe'=2,'dp'=4,'mp'=4] {'dp'}, dimensions={0} | all-to-all | bytes 524288 | tf_op jit(solution)/shard_map/all_to_all | solution.py:79
  386.9 25.8 %all-gather.16.cloned.1.call-done = bf16[256,4096]{1,0:T(8,128)(2,1)} async-done(((bf16[32,4096]{1,0:T(8,128)(2,1)}), bf16[256,4096]{1,0:T(8,128)(2,1)}) %all-gather.16.cloned.1.call-update) | async-done | bytes 2097168 | tf_op jit(solution)/shard_map/all_gather | solution.py:83
  412.7 17.5 %fusion.38 = (f32[256]{0:T(256)S(1)}, f32[256,4096]{1,0:T(8,128)}) fusion(bf16[256,4096]{1,0:T(8,128)(2,1)} %all-gather.16.cloned.1.call-done, bf16[4096,4096]{1,0:T(8,128)(2,1)} %param.15), kind=kOutput, calls=%fused_computation.83 | convolution fusion | flops 8590983168 | bytes 39846912 | tf_op jit(solution)/shard_map/dot_general | solution.py:84
  430.2 3.5 exponential_reduce_fusion
  433.7 23.4 %all-gather.1 = f32[8,3,256]{2,1,0:T(4,128)S(1)} all-gather(f32[1,3,256]{2,1,0:T(4,128)S(1)} %maximum_bitcast_fusion), channel_id=2, replica_groups=mesh['pipe'=2,'dp'=4,'mp'=4] {'pipe','mp'}, dimensions={0}, use_global_device_ids=true | all-gather | bytes 27648 | tf_op jit(solution)/shard_map/all_gather | solution.py:93
  457.4 11.7 %psum.23 = f32[4]{0:T(128)S(1)} all-reduce(f32[4]{0:T(128)S(1)} %get-tuple-element.8), channel_id=1, replica_groups=mesh['pipe'=2,'dp'=4,'mp'=4] {'dp'}, use_global_device_ids=true, to_apply=%region_17.18 | all-reduce | flops 4 | bytes 32 | tf_op jit(solution)/shard_map/psum | solution.py:36
  (68 shorter events, 6.8 us)
Async XLA Ops:
  7.2 1.6 copy-start
  7.2 8.9 %copy-start.8 = (f32[1,4096]{1,0:T(1,128)S(1)}, f32[1,4096]{1,0:T(1,128)}, u32[]{:S(2)}) copy-start(f32[1,4096]{1,0:T(1,128)} %param.13) | copy-start | bytes 49156
  9.7 15.3 %all-to-all-start = ((bf16[4,32,1024]{2,1,0:T(8,128)(2,1)}), bf16[4,32,1024]{2,1,0:T(8,128)(2,1)S(1)}, u32[]{:S(2)}, u32[]{:S(2)}) async-start(bf16[4,32,1024]{2,1,0:T(8,128)(2,1)} %copy.22), calls=%async_computation | async-start | bytes 524288 | tf_op jit(solution)/shard_map/all_to_all | solution.py:61
  16.1 45.9 %all-gather.8.cloned.1.call-start = ((), (), s32[]{:S(2)}) async-start(), calls=%async_computation.6 | async-start | bytes 2359296 | tf_op jit(solution)/shard_map/all_gather | solution.py:70
  16.1 1.2 collective-permute-start
  35.9 72.0 %reduce-scatter.5.cloned.1.call-start = ((), (), s32[]{:S(2)}) async-start(), calls=%async_computation.7 | async-start | bytes 2293760 | tf_op jit(solution)/shard_map/reduce_scatter | solution.py:72
  37.6 4.0 collective-permute-start.1
  67.8 82.7 %all-gather.10.cloned.1.call-start = ((), (), s32[]{:S(2)}) async-start(), calls=%async_computation.8 | async-start | bytes 2293760 | tf_op jit(solution)/shard_map/all_gather | solution.py:74
  110.0 86.5 %reduce-scatter.7.cloned.1.call-start = ((), (), s32[]{:S(2)}) async-start(), calls=%async_computation.9 | async-start | bytes 2359296 | tf_op jit(solution)/shard_map/reduce_scatter | solution.py:76
  111.7 4.0 collective-permute-start.2
  156.3 80.0 %all-gather.12.cloned.1.call-start = ((), (), s32[]{:S(2)}) async-start(), calls=%async_computation.10 | async-start | bytes 2359296 | tf_op jit(solution)/shard_map/all_gather | solution.py:70
  211.1 71.1 %reduce-scatter.9.cloned.1.call-start = ((), (), s32[]{:S(2)}) async-start(), calls=%async_computation.11 | async-start | bytes 2293760 | tf_op jit(solution)/shard_map/reduce_scatter | solution.py:72
  242.6 82.3 %all-gather.14.cloned.1.call-start = ((), (), s32[]{:S(2)}) async-start(), calls=%async_computation.12 | async-start | bytes 2293760 | tf_op jit(solution)/shard_map/all_gather | solution.py:74
  284.4 86.9 %reduce-scatter.11.cloned.1.call-start = ((), (), s32[]{:S(2)}) async-start(), calls=%async_computation.13 | async-start | bytes 2359296 | tf_op jit(solution)/shard_map/reduce_scatter | solution.py:76
  331.2 40.1 %copy-start.2 = (bf16[128,1024]{1,0:T(8,128)(2,1)S(1)}, bf16[128,1024]{1,0:T(8,128)(2,1)}, u32[]{:S(2)}) copy-start(bf16[128,1024]{1,0:T(8,128)(2,1)} %reduce-scatter.7.cloned.1.call-done) | copy-start | bytes 786436
  331.2 54.6 %copy-start.3 = (f32[4096]{0:T(1024)S(1)}, f32[4096]{0:T(1024)}, u32[]{:S(2)}) copy-start(f32[4096]{0:T(1024)} %param.14) | copy-start | bytes 49156
  331.2 81.5 %all-gather.16.cloned.1.call-start = ((), (), s32[]{:S(2)}) async-start(), calls=%async_computation.14 | async-start | bytes 2359296 | tf_op jit(solution)/shard_map/all_gather | solution.py:83
  372.4 14.3 %copy-start.9 = (s32[1,4]{1,0:T(1,128)S(1)}, s32[1,4]{1,0:T(1,128)}, u32[]{:S(2)}) copy-start(s32[1,4]{1,0:T(1,128)} %param.19) | copy-start | bytes 52
  372.4 14.5 %copy-start.5 = (s32[4,64]{1,0:T(4,128)S(1)}, s32[4,64]{1,0:T(4,128)}, u32[]{:S(2)}) copy-start(s32[4,64]{1,0:T(4,128)} %param.16) | copy-start | bytes 3076
  430.2 40.2 %copy-start.1 = (bf16[4,64,4096]{2,1,0:T(8,128)(2,1)S(1)}, bf16[4,64,4096]{2,1,0:T(8,128)(2,1)}, u32[]{:S(2)}) copy-start(bf16[4,64,4096]{2,1,0:T(8,128)(2,1)} %param.10) | copy-start | bytes 6291460
  430.2 27.0 %copy-start.6 = (f32[4,64]{1,0:T(4,128)S(1)}, f32[4,64]{1,0:T(4,128)}, u32[]{:S(2)}) copy-start(f32[4,64]{1,0:T(4,128)} %param.18) | copy-start | bytes 3076
  430.2 27.0 %copy-start.7 = (s32[4,64]{1,0:T(4,128)S(1)}, s32[4,64]{1,0:T(4,128)}, u32[]{:S(2)}) copy-start(s32[4,64]{1,0:T(4,128)} %param.17) | copy-start | bytes 3076
  457.2 13.1 %copy-start.4 = (f32[4,64]{1,0:T(4,128)}, f32[4,64]{1,0:T(4,128)S(1)}, u32[]{:S(2)}) copy-start(f32[4,64]{1,0:T(4,128)S(1)} %sub.63) | copy-start | bytes 3076
Sparse Core Ops, SparseCore 0:
  36.0 26.0 all-gather.7
  67.9 39.9 reduce-scatter.4
  110.1 40.3 all-gather.9
  156.4 40.0 reduce-scatter.6
  211.2 24.9 all-gather.11
  242.7 39.4 reduce-scatter.8
  284.5 40.3 all-gather.13
  331.4 39.9 reduce-scatter.10
  386.8 25.8 all-gather.15

commit v2 on v1

--- a/solution.py
+++ b/solution.py
@@ -1,6 +1,9 @@
+import functools
 import jax
 import jax.numpy as jnp
 from jax import lax
+from jax.experimental import pallas as pl
+from jax.experimental.pallas import tpu as pltpu
 from jax.sharding import PartitionSpec as P
 
 SEQ_MB = 1
@@ -8,6 +11,348 @@
 epsilon = 1e-05
 ipo_tau = 0.5
 VP = ("pipe", "mp")
+MESH = pl.DeviceIdType.MESH
+PIECES = 8
+
+
+def remote(src, dst, send_sem, recv_sem, target):
+    return pltpu.make_async_remote_copy(
+        src_ref=src,
+        dst_ref=dst,
+        send_sem=send_sem,
+        recv_sem=recv_sem,
+        device_id=target,
+        device_id_type=MESH,
+    )
+
+
+def greet(axes):
+    barrier = pltpu.get_barrier_semaphore()
+    total = 0
+    for axis in axes:
+        size = lax.axis_size(axis)
+        here = lax.axis_index(axis)
+        for k in range(1, size):
+            pl.semaphore_signal(
+                barrier, inc=1, device_id={axis: lax.rem(here + k, size)}, device_id_type=MESH
+            )
+        total += size - 1
+    pl.semaphore_wait(barrier, total)
+
+
+def chunk_rows(index, size):
+    return pl.ds(pl.multiple_of(index * size, 8), size)
+
+
+def spread(full, size, mp_sems, pipe_sems):
+    (mp_send, mp_recv), (pipe_send, pipe_recv) = mp_sems, pipe_sems
+    count = lax.axis_size("mp")
+    m, p = lax.axis_index("mp"), lax.axis_index("pipe")
+
+    def to_mp(k, owner):
+        rows = full.at[chunk_rows(p * count + owner, size)]
+        return remote(rows, rows, mp_send.at[k], mp_recv.at[k], {"mp": lax.rem(m + k, count)})
+
+    def to_pipe(k, pipe):
+        rows = full.at[chunk_rows(pipe * count + lax.rem(m - k + count, count), size)]
+        return remote(rows, rows, pipe_send.at[k], pipe_recv.at[k], {"pipe": 1 - p})
+
+    for k in range(1, count):
+        to_mp(k, m).start()
+    to_pipe(0, p).start()
+    for k in range(1, count):
+        to_mp(k, lax.rem(m - k + count, count)).wait_recv()
+        to_pipe(k, p).start()
+    for k in range(count):
+        to_pipe(k, 1 - p).wait_recv()
+    for k in range(1, count):
+        to_mp(k, m).wait_send()
+    for k in range(count):
+        to_pipe(k, p).wait_send()
+
+
+def gather_sum(part, size, near, far, sent, sems):
+    near_send, near_recv, far_send, far_recv = sems
+    count = lax.axis_size("mp")
+    m, p = lax.axis_index("mp"), lax.axis_index("pipe")
+    order = list(range(1, count)) + [0]
+
+    def to_core(k):
+        rows = part.at[chunk_rows((1 - p) * count + lax.rem(m + k, count), size)]
+        return remote(rows, near.at[k], near_send.at[k], near_recv.at[k], {"pipe": 1 - p})
+
+    def to_chip(k):
+        return remote(
+            sent.at[k], far.at[k], far_send.at[k], far_recv.at[k], {"mp": lax.rem(m + k, count)}
+        )
+
+    for k in order:
+        to_core(k).start()
+    for k in order:
+        to_core(k).wait_recv()
+        own = part[chunk_rows(p * count + lax.rem(m + k, count), size), :].astype(jnp.float32)
+        own = own + near[k].astype(jnp.float32)
+        if k > 0:
+            sent[k] = own.astype(sent.dtype)
+            to_chip(k).start()
+    for k in range(1, count):
+        to_chip(k).wait_recv()
+        own = own + far[k].astype(jnp.float32)
+    for k in range(1, count):
+        to_chip(k).wait_send()
+    for k in order:
+        to_core(k).wait_send()
+    return own
+
+
+def share_sum(slots, send, recv):
+    count = lax.axis_size("dp")
+    d = lax.axis_index("dp")
+
+    def hop(k):
+        return remote(
+            slots.at[0], slots.at[k], send.at[k], recv.at[k], {"dp": lax.rem(d + k, count)}
+        )
+
+    for k in range(1, count):
+        hop(k).start()
+    total = slots[0]
+    for k in range(1, count):
+        hop(k).wait_recv()
+        total = total + slots[k]
+    for k in range(1, count):
+        hop(k).wait_send()
+    return total
+
+
+def first_kernel(
+    x_ref, gain_ref, blocks_ref, full_ref, normed_ref, n_send, n_recv, x_send, x_recv, ms, mr, ps, pr
+):
+    count = lax.axis_size("dp")
+    d = lax.axis_index("dp")
+    v = lax.axis_index(("pipe", "mp"))
+    part, width = x_ref.shape
+    block = width // count
+    greet(("dp", "mp", "pipe"))
+    wide = x_ref[...].astype(jnp.float32)
+    scale = lax.rsqrt(jnp.mean(wide * wide, axis=-1, keepdims=True) + epsilon)
+    normed_ref[...] = (wide * scale * gain_ref[...]).astype(normed_ref.dtype)
+
+    def columns(owner):
+        return pl.ds(pl.multiple_of(owner * block, 128), block)
+
+    def normed_hop(k, owner):
+        to = lax.rem(d + k, count)
+        return remote(
+            normed_ref.at[:, columns(to)],
+            full_ref.at[chunk_rows(v * count + owner, part)],
+            n_send.at[k],
+            n_recv.at[k],
+            {"dp": to},
+        )
+
+    def plain_hop(k, owner):
+        to = lax.rem(d + k, count)
+        return remote(
+            x_ref.at[:, columns(to)],
+            blocks_ref.at[chunk_rows(owner, part)],
+            x_send.at[k],
+            x_recv.at[k],
+            {"dp": to},
+        )
+
+    for k in range(1, count):
+        normed_hop(k, d).start()
+    for k in range(1, count):
+        plain_hop(k, d).start()
+    full_ref[chunk_rows(v * count + d, part), :] = normed_ref[:, columns(d)]
+    blocks_ref[chunk_rows(d, part), :] = x_ref[:, columns(d)]
+    for k in range(1, count):
+        normed_hop(k, lax.rem(d - k + count, count)).wait_recv()
+    spread(full_ref, part * count, (ms, mr), (ps, pr))
+    for k in range(1, count):
+        plain_hop(k, lax.rem(d - k + count, count)).wait_recv()
+    for k in range(1, count):
+        normed_hop(k, d).wait_send()
+        plain_hop(k, d).wait_send()
+
+
+def middle_kernel(
+    width, part_ref, resid_ref, gain_ref, blocks_ref, full_ref,
+    near, far, sent, slots, ns, nr, fs, fr, qs, qr, ms, mr, ps, pr,
+):
+    v = lax.axis_index(("pipe", "mp"))
+    size = resid_ref.shape[0]
+    greet(("dp", "mp", "pipe"))
+    summed = gather_sum(part_ref, size, near, far, sent, (ns, nr, fs, fr))
+    value = (resid_ref[...].astype(jnp.float32) + summed).astype(jnp.bfloat16)
+    blocks_ref[...] = value
+    wide = value.astype(jnp.float32)
+    slots[0] = lax.dot_general(
+        jnp.ones((8, wide.shape[1]), jnp.float32),
+        wide * wide,
+        (((1,), (1,)), ((), ())),
+        precision=lax.Precision.HIGHEST,
+        preferred_element_type=jnp.float32,
+    )
+    scale = lax.rsqrt(share_sum(slots, qs, qr) / width + epsilon)
+    scale = jnp.transpose(scale)[:, :1]
+    wide = blocks_ref[...].astype(jnp.float32)
+    full_ref[chunk_rows(v, size), :] = (wide * scale * gain_ref[...]).astype(full_ref.dtype)
+    spread(full_ref, size, (ms, mr), (ps, pr))
+
+
+def last_kernel(
+    part_ref, resid_ref, gain_ref, full_ref,
+    near, far, sent, blocks, fin, ns, nr, fs, fr, hs, hr, ms, mr, ps, pr,
+):
+    count = lax.axis_size("dp")
+    d = lax.axis_index("dp")
+    v = lax.axis_index(("pipe", "mp"))
+    size, block = resid_ref.shape
+    part = size // count
+    greet(("dp", "mp", "pipe"))
+    summed = gather_sum(part_ref, size, near, far, sent, (ns, nr, fs, fr))
+    blocks[...] = (resid_ref[...].astype(jnp.float32) + summed).astype(jnp.bfloat16)
+
+    def hop(k, owner):
+        to = lax.rem(d + k, count)
+        return remote(
+            blocks.at[chunk_rows(to, part)], fin.at[owner], hs.at[k], hr.at[k], {"dp": to}
+        )
+
+    for k in range(1, count):
+        hop(k, d).start()
+    fin[d] = blocks[chunk_rows(d, part), :]
+    for k in range(1, count):
+        hop(k, lax.rem(d - k + count, count)).wait_recv()
+    total = 0.0
+    for g in range(count):
+        wide = fin[g].astype(jnp.float32)
+        total = total + jnp.sum(wide * wide, axis=1, keepdims=True)
+    scale = lax.rsqrt(total / (block * count) + epsilon)
+    for g in range(count):
+        cut = slice(g * block, (g + 1) * block)
+        full_ref[chunk_rows(v, part), cut] = (
+            fin[g].astype(jnp.float32) * scale * gain_ref[:, cut]
+        ).astype(full_ref.dtype)
+    spread(full_ref, part, (ms, mr), (ps, pr))
+    for k in range(1, count):
+        hop(k, d).wait_send()
+
+
+def stats_kernel(stats_ref, counts_ref, full_ref, total_ref, slots, qs, qr, ms, mr, ps, pr):
+    v = lax.axis_index(("pipe", "mp"))
+    size = stats_ref.shape[0]
+    greet(("dp", "mp", "pipe"))
+    slots[0] = counts_ref[...]
+    full_ref[chunk_rows(v, size), :] = stats_ref[...]
+    total_ref[...] = share_sum(slots, qs, qr)
+    spread(full_ref, size, (ms, mr), (ps, pr))
+
+
+def chain_kernel(h_ref, out_ref, arrived, summed, rs, rr, gs, gr):
+    count = lax.axis_size("dp")
+    d = lax.axis_index("dp")
+    half = h_ref.shape[0] // 2
+    rows = half // PIECES
+    right, left = lax.rem(d + 1, count), lax.rem(d + count - 1, count)
+    barrier = pltpu.get_barrier_semaphore()
+    for has, who in ((d > 0, left), (d < count - 1, right)):
+
+        @pl.when(has)
+        def _():
+            pl.semaphore_signal(barrier, inc=1, device_id={"dp": who}, device_id_type=MESH)
+
+    ends = (d > 0).astype(jnp.int32) + (d < count - 1).astype(jnp.int32)
+    pl.semaphore_wait(barrier, ends)
+
+    hops = (d, count - 1 - d)
+
+    def cut(way, c):
+        return pl.ds(pl.multiple_of((1 - way) * half + c * rows, 16), rows)
+
+    def onward_copy(way, c, source):
+        to = (right, left)[way]
+        return remote(source, arrived.at[way, c], rs.at[way, c], rr.at[way, c], {"dp": to})
+
+    def back_copy(way, c):
+        spot = out_ref.at[cut(way, c)]
+        to = (left, right)[way]
+        return remote(spot, spot, gs.at[way, c], gr.at[way, c], {"dp": to})
+
+    for way in range(2):
+
+        @pl.when(hops[way] == 0)
+        def _():
+            for c in range(PIECES):
+                onward_copy(way, c, h_ref.at[cut(way, c)]).start()
+
+    def step(t, carry):
+        for way in range(2):
+            before = hops[way]
+            c = t - before
+
+            @pl.when((before > 0) & (c >= 0) & (c < PIECES))
+            def _():
+                onward_copy(way, c, summed.at[way, c]).wait_recv()
+                total = arrived[way, c] + h_ref[cut(way, c), :]
+
+                @pl.when(before < count - 1)
+                def _():
+                    summed[way, c] = total
+                    onward_copy(way, c, summed.at[way, c]).start()
+
+                @pl.when(before == count - 1)
+                def _():
+                    out_ref[cut(way, c), :] = (total / (1.0 + jnp.exp(-total))).astype(
+                        out_ref.dtype
+                    )
+                    back_copy(way, c).start()
+
+        for way in range(2):
+            after = count - 1 - hops[way]
+            g = t - (count - 1) - after
+
+            @pl.when((after > 0) & (g >= 0) & (g < PIECES))
+            def _():
+                back_copy(way, g).wait_recv()
+
+                @pl.when(after < count - 1)
+                def _():
+                    back_copy(way, g).start()
+
+        return carry
+
+    lax.fori_loop(0, PIECES + 2 * (count - 1), step, 0)
+    for way in range(2):
+
+        @pl.when(hops[way] < count - 1)
+        def _():
+            for c in range(PIECES):
+                onward_copy(way, c, summed.at[way, c]).wait_send()
+
+        @pl.when(hops[way] > 0)
+        def _():
+            for c in range(PIECES):
+                back_copy(way, c).wait_send()
+
+
+def call(kernel, name, ident, outs, scratch, *args):
+    spec = pl.BlockSpec(memory_space=pltpu.VMEM)
+    return pl.pallas_call(
+        kernel,
+        name=name,
+        out_shape=outs,
+        in_specs=[spec] * len(args),
+        out_specs=jax.tree.map(lambda _: spec, outs),
+        scratch_shapes=scratch,
+        compiler_params=pltpu.CompilerParams(collective_id=ident, has_side_effects=True),
+    )(*args)
+
+
+def sems(*shape):
+    return [pltpu.SemaphoreType.DMA(shape)] * 2
 
 
 def shards(
@@ -33,7 +378,11 @@
     block = model_width // groups
     mask_values = response_masks.astype(jnp.float32)
     local_counts = jnp.sum(mask_values, axis=1)
-    counts = lax.psum(local_counts, "dp")
+    count = lax.axis_size("mp")
+    bf16 = jnp.bfloat16
+    spread_sems = sems(count) + sems(count)
+    reach_sems = sems(count) + sems(count)
+    buffers = [pltpu.VMEM((count, part, block), jnp.float32) for part in [rows // vp_size * groups]] * 3
 
     up_own, down_own = up_weight[0], down_weight[0]
     half = up_own.shape[1] // 2
@@ -58,29 +407,67 @@
     mine = lax.dynamic_slice_in_dim(
         hidden_states.reshape(rows, model_width), vp_index * part, part, 0
     )
-    blocks = lax.all_to_all(
-        mine.reshape(part, groups, block).transpose(1, 0, 2), "dp", 0, 0, tiled=True
-    ).reshape(groups * part, block)
-
+    size = part * groups
+    total_rows = rows * groups
+    blocks, full = call(
+        first_kernel,
+        "first",
+        0,
+        [
+            jax.ShapeDtypeStruct((size, block), bf16),
+            jax.ShapeDtypeStruct((total_rows, block), bf16),
+        ],
+        [pltpu.VMEM((part, model_width), bf16)] + sems(groups) + sems(groups) + spread_sems,
+        mine,
+        jnp.where(pipe_index == 0, layer_gain, gain_other),
+    )
     for s in range(2):
         gain, up, down = section_of(s)
-        wide = blocks.astype(jnp.float32)
-        total = lax.psum(jnp.sum(wide * wide, axis=1, keepdims=True), "dp")
-        normed = (wide * lax.rsqrt(total / model_width + epsilon) * gain).astype(jnp.bfloat16)
-        full = lax.all_gather(normed, VP, axis=0, tiled=True)
-        hidden = jnp.dot(full, up, preferred_element_type=jnp.float32).astype(jnp.bfloat16)
-        hidden = lax.psum_scatter(hidden, "dp", scatter_dimension=0, tiled=True)
-        active = jax.nn.silu(hidden.astype(jnp.float32)).astype(jnp.bfloat16)
-        active = lax.all_gather(active, "dp", axis=0, tiled=True)
-        out = jnp.dot(active, down, preferred_element_type=jnp.float32).astype(jnp.bfloat16)
-        out = lax.psum_scatter(out, VP, scatter_dimension=0, tiled=True)
-        blocks = (wide + out.astype(jnp.float32)).astype(jnp.bfloat16)
-
-    finals = lax.all_to_all(blocks.reshape(groups, part, block), "dp", 0, 0, tiled=True)
-    finals = finals.transpose(1, 0, 2).reshape(part, model_width).astype(jnp.float32)
-    mean_square = jnp.mean(finals * finals, axis=-1, keepdims=True)
-    normed_final = (finals * lax.rsqrt(mean_square + epsilon) * final_gain).astype(jnp.bfloat16)
-    normed_final = lax.all_gather(normed_final, VP, axis=0, tiled=True)
+        hidden = jnp.dot(full, up, preferred_element_type=jnp.float32)
+        piece = hidden.shape[0] // (2 * PIECES)
+        active = call(
+            chain_kernel,
+            "chain",
+            1,
+            jax.ShapeDtypeStruct(hidden.shape, bf16),
+            [pltpu.VMEM((2, PIECES, piece, half), jnp.float32)] * 2 + sems(2, PIECES) + sems(2, PIECES),
+            hidden,
+        )
+        out = jnp.dot(active, down, preferred_element_type=jnp.float32)
+        if s == 0:
+            gain = section_of(1)[0]
+            blocks, full = call(
+                functools.partial(middle_kernel, model_width),
+                "middle",
+                2,
+                [
+                    jax.ShapeDtypeStruct((size, block), bf16),
+                    jax.ShapeDtypeStruct((total_rows, block), bf16),
+                ],
+                buffers
+                + [pltpu.VMEM((groups, 8, size), jnp.float32)]
+                + reach_sems
+                + sems(groups)
+                + spread_sems,
+                out,
+                blocks,
+                gain[None],
+            )
+        else:
+            normed_final = call(
+                last_kernel,
+                "last",
+                3,
+                jax.ShapeDtypeStruct((rows, model_width), bf16),
+                buffers
+                + [pltpu.VMEM((size, block), bf16), pltpu.VMEM((groups, part, block), bf16)]
+                + reach_sems
+                + sems(groups)
+                + spread_sems,
+                out,
+                blocks,
+                final_gain[None],
+            )
     logits = lax.dot_general(
         normed_final, unembedding, (((1,), (1,)), ((), ())), preferred_element_type=jnp.float32
     )
@@ -90,7 +477,22 @@
     picked = jnp.sum(jnp.where(columns == local_ids[:, None], logits, 0.0), axis=1)
     local_top = jnp.max(logits, axis=1)
     local_sum = jnp.sum(jnp.exp(logits - local_top[:, None]), axis=1)
-    stats = lax.all_gather(jnp.stack([local_top, local_sum, picked]), VP, axis=0)
+    stats = jnp.pad(jnp.stack([local_top, local_sum, picked]), ((0, 5), (0, 0)))
+    padded = jnp.pad(local_counts[None], ((0, 7), (0, -seq_count % 128)))
+    stats, counts = call(
+        stats_kernel,
+        "stats",
+        4,
+        [
+            jax.ShapeDtypeStruct((vp_size * 8, rows), jnp.float32),
+            jax.ShapeDtypeStruct(padded.shape, jnp.float32),
+        ],
+        [pltpu.VMEM((groups,) + padded.shape, jnp.float32)] + sems(groups) + spread_sems,
+        stats,
+        padded,
+    )
+    stats = stats.reshape(vp_size, 8, rows)
+    counts = counts[0, :seq_count]
     top_value = jnp.max(stats[:, 0], axis=0)
     exp_total = jnp.sum(stats[:, 1] * jnp.exp(stats[:, 0] - top_value), axis=0)
     picked_all = jnp.sum(stats[:, 2], axis=0)

time: 478 us -> 407 us (0.85)
  Pallas kernels: 0 us -> 345 us
  waiting for transfers between devices: 323 us -> 0.01 us
  blocking collectives: 69.7 us -> 0 us
  between operations: 14 us -> 0.74 us
  other arithmetic: 15.1 us -> 9.22 us
  starting transfers between devices: 6.89 us -> 1.13 us
    pallas_call x0 -> x6, Pallas kernels: none -> 345 us  [call(): pl.pallas_call(kernel, name=name, out_shape=outs, in_specs=[spec] * len(a...]
    reduce_scatter x4 -> x0, waiting for transfers between devices: 160 us -> none  [the longest x2 80.2 us: shards(): out = lax.psum_scatter(out, VP, scatter_dimension=0, tiled=True)]
    all_gather x5 -> x0, waiting for transfers between devices: 147 us -> none  [the longest x2 75.3 us: shards(): active = lax.all_gather(active, 'dp', axis=0, tiled=True)]
    psum x3 -> x0, blocking collectives: 33.2 us -> none  [the longest x2 21.5 us: shards(): total = lax.psum(jnp.sum(wide * wide, axis=1, keepdims=True), 'dp')]
    all_gather x1 -> x0, blocking collectives: 23.4 us -> none  [shards(): lax.all_gather(jnp.stack([local_top, local_sum, picked]), VP, axis=0)]
    all_to_all x1 -> x0, blocking collectives: 13.1 us -> none  [shards(): lax.all_to_all(blocks.reshape(groups, part, block), 'dp', 0, 0, tiled=True)]
    convert_element_type x6 -> x0, other arithmetic: 8.64 us -> none  [the longest x2 4.13 us: shards(): active = jax.nn.silu(hidden.astype(jnp.float32)).astype(jnp.bfloat16)]
    all_to_all x1 -> x0, waiting for transfers between devices: 7.65 us -> none  [shards(): lax.all_to_all(mine.reshape(part, groups, block).transpose(1, 0, 2), 'dp'...]
  transfers between devices with their start and end apart: 13 -> 3, of which waited for: 13 -> 0; matrix products, arithmetic and copies ran while one was open for 1% -> 3% of each run, Pallas kernels for 0% -> 32%
where the time goes in v2:
time: 407 us
  Pallas kernels  345 us (85%)
  matrix products  43.9 us (11%)
  other arithmetic  9.22 us (2%)
  local copies, waits for them, and re-layouts  6.13 us (2%)
    pallas_call x6, Pallas kernels, call(): pl.pallas_call(kernel, name=name, out_shape=outs, in_specs=[spec] * len(a...  345 us
    dot_general x1, matrix products, shards(): lax.dot_general(normed_final, unembedding, (((1,), (1,)), ((), ())), pref...  17.5 us
    dot_general x2, matrix products, shards(): out = jnp.dot(active, down, preferred_element_type=jnp.float32)  13.3 us
    dot_general x2, matrix products, shards(): hidden = jnp.dot(full, up, preferred_element_type=jnp.float32)  13.2 us
  transfers between devices with their start and end apart: 3, of which 0 were waited for; matrix products, arithmetic and copies ran while one was open for 3% of the time, Pallas kernels for 32%

profile of v2, /device:TPU:0, one launch (start us, length us, event | category | flops | bytes accessed | tf_op | source)
XLA Modules:
  0.0 406.7 jit_solution(17871407408044581722)
XLA Ops:
  0.6 0.6 collective-permute-start
  1.2 3.0 dynamic-slice_bitcast_fusion.1
  4.3 0.1 collective-permute-start.1
  4.4 1.4 dynamic-slice_bitcast_fusion
  5.8 0.5 collective-permute-start.2
  6.2 0.7 constant_dynamic-slice_fusion.x_ref
  7.0 0.1 convert_reduce_fusion
  7.1 0.1 slice.23
  7.2 0.1 slice.24
  7.4 0.6 pad.9.counts_ref
  8.0 0.6 broadcast_select_fusion.gain_ref
  8.6 28.2 %first.1 = (bf16[128,1024]{1,0:T(8,128)(2,1)}, bf16[1024,1024]{1,0:T(8,128)(2,1)}) custom-call(bf16[32,4096]{1,0:T(8,128)(2,1)} %constant_dynamic-slice_fusion.x_ref, f32[1,4096]{1,0:T(1,128)} %broadcast_select_fusion.gain_ref), custom_call_target="tpu_custom_call" | custom-call | tf_op jit(solution)/shard_map/first/pallas_call | solution.py:343
  36.7 0.6 broadcast_select_fusion.1.gain_ref
  37.4 6.3 %fusion.2.h_ref = f32[1024,896]{1,0:T(8,128)} fusion(bf16[1024,1024]{1,0:T(8,128)(2,1)} %get-tuple-element.9, bf16[1024,896]{1,0:T(8,128)(2,1)} %collective-permute-done.1, pred[]{:T(512)S(6)} %eq.46, bf16[1,1024,1792]{2,1,0:T(8,128)(2,1)} %param.11, s32[]{:T(128)S(6)} %select_n.74), kind=kOutput, calls=%fused_computation.9 | convolution fusion | flops 1879965696 | bytes 9437189 | tf_op jit(solution)/shard_map/dot_general | solution.py:426
  43.6 102.4 %chain.2 = bf16[1024,896]{1,0:T(8,128)(2,1)} custom-call(f32[1024,896]{1,0:T(8,128)} %fusion.2.h_ref), custom_call_target="tpu_custom_call" | custom-call | tf_op jit(solution)/shard_map/chain/pallas_call | solution.py:343
  146.1 6.4 %fusion.part_ref = f32[1024,1024]{1,0:T(8,128)} fusion(bf16[1024,896]{1,0:T(8,128)(2,1)} %chain.2, bf16[896,1024]{1,0:T(8,128)(2,1)} %collective-permute-done.2, pred[]{:T(512)S(6)} %eq.46, bf16[1,1792,1024]{2,1,0:T(8,128)(2,1)} %param.12, s32[]{:T(128)S(6)} %select_n.74), kind=kOutput, calls=%fused_computation.5 | convolution fusion | flops 1879965696 | bytes 9699333 | tf_op jit(solution)/shard_map/dot_general | solution.py:436
  152.4 51.1 %middle.1 = (bf16[128,1024]{1,0:T(8,128)(2,1)}, bf16[1024,1024]{1,0:T(8,128)(2,1)}) custom-call(f32[1024,1024]{1,0:T(8,128)} %fusion.part_ref, bf16[128,1024]{1,0:T(8,128)(2,1)} %get-tuple-element.10.resid_ref, f32[1,1024]{1,0:T(1,128)} %broadcast_select_fusion.1.gain_ref), custom_call_target="tpu_custom_call" | custom-call | tf_op jit(solution)/shard_map/middle/pallas_call | solution.py:343
  203.5 6.9 %fusion.3.h_ref = f32[1024,896]{1,0:T(8,128)} fusion(bf16[1024,1024]{1,0:T(8,128)(2,1)} %get-tuple-element.11, bf16[1024,896]{1,0:T(8,128)(2,1)} %collective-permute-done.1, pred[]{:T(512)S(6)} %eq.47, bf16[1,1024,1792]{2,1,0:T(8,128)(2,1)} %param.11, s32[]{:T(128)S(6)} %select_n.74), kind=kOutput, calls=%fused_computation.10 | convolution fusion | flops 1879965696 | bytes 9437189 | tf_op jit(solution)/shard_map/dot_general | solution.py:426
  210.4 98.7 %chain.3 = bf16[1024,896]{1,0:T(8,128)(2,1)} custom-call(f32[1024,896]{1,0:T(8,128)} %fusion.3.h_ref), custom_call_target="tpu_custom_call" | custom-call | tf_op jit(solution)/shard_map/chain/pallas_call | solution.py:343
  309.1 6.9 %fusion.1.part_ref = f32[1024,1024]{1,0:T(8,128)} fusion(bf16[1024,896]{1,0:T(8,128)(2,1)} %chain.3, bf16[896,1024]{1,0:T(8,128)(2,1)} %collective-permute-done.2, pred[]{:T(512)S(6)} %eq.47, bf16[1,1792,1024]{2,1,0:T(8,128)(2,1)} %param.12, s32[]{:T(128)S(6)} %select_n.74), kind=kOutput, calls=%fused_computation.6 | convolution fusion | flops 1879965696 | bytes 9699333 | tf_op jit(solution)/shard_map/dot_general | solution.py:436
  316.0 53.0 %last.1 = bf16[256,4096]{1,0:T(8,128)(2,1)} custom-call(f32[1024,1024]{1,0:T(8,128)} %fusion.1.part_ref, bf16[128,1024]{1,0:T(8,128)(2,1)} %get-tuple-element.12.resid_ref, f32[1,4096]{1,0:T(1,128)} %bitcast.58), custom_call_target="tpu_custom_call" | custom-call | tf_op jit(solution)/shard_map/last/pallas_call | solution.py:343
  369.0 17.5 %fusion.24 = (f32[256]{0:T(256)S(1)}, f32[256,4096]{1,0:T(8,128)}) fusion(bf16[256,4096]{1,0:T(8,128)(2,1)} %last.1, bf16[4096,4096]{1,0:T(8,128)(2,1)} %param.15), kind=kOutput, calls=%fused_computation.54 | convolution fusion | flops 8590983168 | bytes 39846912 | tf_op jit(solution)/shard_map/dot_general | solution.py:471
  386.5 3.5 exponential_reduce_fusion
  390.0 0.6 select_maximum_fusion.stats_ref
  390.6 12.2 %stats.1 = (f32[64,256]{1,0:T(8,128)}, f32[8,128]{1,0:T(8,128)}) custom-call(f32[8,256]{1,0:T(8,128)} %select_maximum_fusion.stats_ref, f32[8,128]{1,0:T(8,128)} %pad.9.counts_ref), custom_call_target="tpu_custom_call" | custom-call | tf_op jit(solution)/shard_map/stats/pallas_call | solution.py:343
  402.7 1.0 slice_reduce_fusion
  403.8 0.1 sub.64
  403.9 0.1 multiply_reduce_fusion
  404.0 1.2 bitcast_divide_fusion.2
  405.2 0.7 fusion.23
  405.9 0.2 fusion.21
  406.1 0.5 add_multiply_fusion
  (25 shorter events, 0.2 us)
Async XLA Ops:
  0.6 5.6 %copy-start = (bf16[4,64,4096]{2,1,0:T(8,128)(2,1)S(1)}, bf16[4,64,4096]{2,1,0:T(8,128)(2,1)}, u32[]{:S(2)}) copy-start(bf16[4,64,4096]{2,1,0:T(8,128)(2,1)} %param.10) | copy-start | bytes 6291460
  0.6 7.3 %collective-permute-start = (f32[1,4096]{1,0:T(1,128)}, f32[1,4096]{1,0:T(1,128)S(1)}, u32[]{:S(2)}, u32[]{:S(2)}) collective-permute-start(f32[1,4096]{1,0:T(1,128)} %param.13), channel_id=1, source_target_pairs={{0,16},{16,0},{1,17},{17,1},{2,18},{18,2},{3,19},{19,3},{4,20},{20... | collective-permute-start | bytes 49160 | tf_op jit(solution)/shard_map/ppermute | solution.py:392
  1.2 3.2 copy-start.2
  4.3 2.7 copy-start.7
  4.3 2.7 copy-start.4
  4.3 2.8 copy-start.8
  4.3 3.7 copy-start.3
  4.3 33.1 %collective-permute-start.1 = (bf16[1024,896]{1,0:T(8,128)(2,1)}, bf16[1024,896]{1,0:T(8,128)(2,1)}, u32[]{:S(2)}, u32[]{:S(2)}) collective-permute-start(bf16[1024,896]{1,0:T(8,128)(2,1)} %dynamic-slice_bitcast_fusion.1), channel_id=1, source_target_pairs={{0,16},{16,0},{1,17},{17,1},{2,18},{18,2},{3,19},{19,3},{4,20},{20... | collective-permute-start | bytes 5505032 | tf_op jit(solution)/shard_map/ppermute | solution.py:393
  5.8 140.3 %collective-permute-start.2 = (bf16[896,1024]{1,0:T(8,128)(2,1)}, bf16[896,1024]{1,0:T(8,128)(2,1)}, u32[]{:S(2)}, u32[]{:S(2)}) collective-permute-start(bf16[896,1024]{1,0:T(8,128)(2,1)} %dynamic-slice_bitcast_fusion), channel_id=1, source_target_pairs={{0,16},{16,0},{1,17},{17,1},{2,18},{18,2},{3,19},{19,3},{4,20},{20... | collective-permute-start | bytes 5505032 | tf_op jit(solution)/shard_map/ppermute | solution.py:394
  386.5 20.2 %copy-start.1 = (bf16[4,64,4096]{2,1,0:T(8,128)(2,1)S(1)}, bf16[4,64,4096]{2,1,0:T(8,128)(2,1)}, u32[]{:S(2)}) copy-start(bf16[4,64,4096]{2,1,0:T(8,128)(2,1)} %param.10) | copy-start | bytes 6291460
  386.5 17.4 %copy-start.6 = (f32[4,64]{1,0:T(4,128)S(1)}, f32[4,64]{1,0:T(4,128)}, u32[]{:S(2)}) copy-start(f32[4,64]{1,0:T(4,128)} %param.18) | copy-start | bytes 3076
  403.9 2.8 copy-start.5
